TPU v7x, 256 devices: a 2x2x32 block of a 4x8x32 slice. The times are simulated.
256 devices in a mesh: tiles: 4 (over y, x), slab: 64 (over z, core).
Axes of the slice: x: 2, y: 2, z: 32, core: 2. Of those that a mesh axis runs over, the one named last changes fastest.
The devices are a block of a 4x8x32 slice.
Arguments:
- transmission: float32 [16384, 4096], P(('tiles', 'slab')), parts along dimension 0, may hold values from -6 to 6
- kernel_spectra: float32 [12, 2, 256, 256], replicated, may hold values from -6 to 6
Outputs:
- resist_image: float32 [16384, 256], P(('tiles', 'slab')), parts along dimension 0
There are 4 independent parts, one for each index of `tiles`. A program takes and returns all parts, laid end to end along the dimension named above; an argument that names none is the same for every part. Nothing has to cross between parts.
All inputs are finite; a program needn't handle non-finite values.
Results may differ from a plain program's by a relative error of at most 0.0001.
Values sent between devices are 32-bit elements; how exact they have to be, the bound alone decides.
A program may use at most 128 MiB of HBM per device.

v0:
```python
import functools
import math

import jax
import jax.numpy as jnp
import numpy as np
from jax import lax
from jax.experimental import pallas as pl
from jax.experimental.pallas import tpu as pltpu
from jax.sharding import PartitionSpec as P

COLS = 256
MESH = pl.DeviceIdType.MESH
F32, BF16 = jnp.float32, jnp.bfloat16
LANES, TILE = 128, 8
SPLIT_ROW = 24

binomial = (0.0625, 0.25, 0.375, 0.25, 0.0625)


def split(x):
    high = x.astype(BF16)
    return high, (x - high.astype(F32)).astype(BF16)


def dot(a, b):
    return lax.dot_general(a, b, (((1,), (0,)), ((), ())), preferred_element_type=F32)


def dot_t(a, b):
    return lax.dot_general(a, b, (((1,), (1,)), ((), ())), preferred_element_type=F32)


def image_kernel(
    sizes,
    t_ref, k_hbm, wy_h, wy_l, tw_chunk, w2_h, w2_l, tw_slab, e_local, ey_h, ey_l, fold, fold_t,
    out_ref,
    k_raw, k_fold, k_row, k_col, k_zero, t_h, t_l, z_ref, slots, part, pair, far, gath,
    e_h, e_l, l_zero, p_zero, q_h, q_l, acc,
    k_sem, s1, r1, s2, r2, s3, r3, sf, rf, rel,
):
    slabs, side, band, nk, rows = sizes
    half = band // 2
    blocks = half // TILE
    near = blocks // 2
    norm = 1.0 / (side * band)

    me = lax.axis_index("slab")
    chip, core = lax.div(me, 2), lax.rem(me, 2)
    own = 2 * lax.rem(chip, near) + core

    def at(step, other=False):
        where = lax.rem(me + 2 * step + slabs, slabs)
        return where + 1 - 2 * core if other else where

    def residue(step, other=False):
        c = 1 - core if other else core
        return 2 * lax.rem(chip + step + slabs, near) + c

    load = pltpu.make_async_copy(k_hbm, k_raw, k_sem)
    load.start()

    barrier = pltpu.get_barrier_semaphore()
    reach = near // 2
    count = 0
    for step in range(-reach, reach + 1):
        for other in (False, True):
            if step or other:
                pl.semaphore_signal(
                    barrier, inc=1, device_id={"slab": at(step, other)}, device_id_type=MESH
                )
                count += 1

    chunks = side // band
    group = 4
    sum_c = jnp.zeros((rows, half), F32)
    sum_s = jnp.zeros((rows, half), F32)
    row_sum = jnp.zeros((rows, LANES), F32)
    for g in range(chunks // group):
        for j in range(group):
            h = g * group + j
            piece = t_ref[:, h * band : (h + 1) * band]
            high, low = split(piece)
            t_h[h * rows : (h + 1) * rows, :] = high
            t_l[h * rows : (h + 1) * rows, :] = low
            row_sum = row_sum + piece[:, :half] + piece[:, half:]
        lo, hi = g * group * rows, (g + 1) * group * rows
        a_h, a_l = t_h[lo:hi, :], t_l[lo:hi, :]
        y = dot(a_h, wy_h[...]) + dot(a_l, wy_h[...]) + dot(a_h, wy_l[...])
        for j in range(group):
            h = g * group + j
            c = y[j * rows : (j + 1) * rows, :half]
            s = y[j * rows : (j + 1) * rows, half:]
            tc, ts = tw_chunk[h : h + 1, :half], tw_chunk[h : h + 1, half:]
            sum_c = sum_c + (c * tc - s * ts)
            sum_s = sum_s + (c * ts + s * tc)
    turned = jnp.transpose(jnp.concatenate([sum_c, sum_s], axis=0))
    column = jnp.sum(row_sum, axis=1, keepdims=True)
    lane = lax.broadcasted_iota(jnp.int32, (rows, LANES), 1)
    row = lax.broadcasted_iota(jnp.int32, (rows, LANES), 0)
    zero_row = jnp.sum(jnp.where(lane == row, column, 0.0), axis=0, keepdims=True)
    z_ref[:, 0:TILE, :] = turned.reshape(blocks, TILE, LANES)
    z_ref[:, TILE : 2 * TILE, :] = jnp.broadcast_to(zero_row[None], (blocks, TILE, LANES))

    pl.semaphore_wait(barrier, count)

    first = []
    for step in sorted(range(1 - reach, reach + 1), key=lambda d: -abs(d)):
        for other in (False, True):
            if not (step or other):
                continue
            n = len(first)
            copy = pltpu.make_async_remote_copy(
                src_ref=z_ref.at[residue(step, other), pl.ds(0, TILE + 1)],
                dst_ref=slots.at[2 * (reach - step) + core, pl.ds(0, TILE + 1)],
                send_sem=s1.at[n],
                recv_sem=r1.at[n],
                device_id={"slab": at(step, other)},
                device_id_type=MESH,
            )
            copy.start()
            first.append(copy)
    pl.semaphore_signal(rel, inc=1, device_id={"slab": at(-reach)}, device_id_type=MESH)

    slots[2 * reach + core] = z_ref[own]

    own_tw = tw_slab[pl.ds(me, 1), :]
    c0, s0 = own_tw[:, :half], own_tw[:, half:]
    ce, se = e_local[:, :half], e_local[:, half:]
    e_own = jnp.concatenate([ce * c0 - se * s0, se * c0 + ce * s0], axis=1)
    high, low = split(e_own)
    e_h[...] = high
    e_l[...] = low

    base = tw_slab[pl.ds(lax.rem(2 * (chip - reach) + slabs, slabs), 1), :]
    bc, bs = base[:, :half], base[:, half:]
    sc, ss = tw_slab[0:blocks, :half], tw_slab[0:blocks, half:]
    wc, ws = bc * sc - bs * ss, bc * ss + bs * sc

    load.wait()
    for copy in first:
        copy.wait_recv()

    k_zero[...] = jnp.zeros_like(k_zero)
    everything = slots[...]
    a_h, a_l = split(everything.reshape(blocks * 2 * TILE, LANES))
    y = dot(a_h, w2_h[...]) + dot(a_l, w2_h[...]) + dot(a_h, w2_l[...])
    cc = jnp.zeros((2 * TILE, half), F32)
    cs = jnp.zeros((2 * TILE, half), F32)
    sc2 = jnp.zeros((TILE, half), F32)
    ss2 = jnp.zeros((TILE, half), F32)
    total = jnp.zeros((2 * TILE, LANES), F32)
    for s in range(blocks):
        lo = s * 2 * TILE
        c, n = y[lo : lo + 2 * TILE, :half], y[lo : lo + 2 * TILE, half:band]
        c2, n2 = y[lo : lo + TILE, band : band + half], y[lo : lo + TILE, band + half :]
        tc, ts = wc[s : s + 1], ws[s : s + 1]
        cc = cc + (c * tc - n * ts)
        cs = cs + (c * ts + n * tc)
        sc2 = sc2 + (c2 * tc - n2 * ts)
        ss2 = ss2 + (c2 * ts + n2 * tc)
        total = total + everything[s]
    lane = lax.broadcasted_iota(jnp.int32, (TILE, LANES), 1)
    row = lax.broadcasted_iota(jnp.int32, (TILE, LANES), 0)
    left = lane < rows
    col_c = jnp.sum(jnp.where(left, total[:TILE], 0.0), axis=1, keepdims=True)
    col_s = jnp.sum(jnp.where(left, 0.0, total[:TILE]), axis=1, keepdims=True)
    both = jnp.sum(jnp.where(left, total[TILE:], 0.0), axis=1, keepdims=True)
    spot = lane == row + TILE * own
    row_c = jnp.sum(jnp.where(spot, col_c, 0.0), axis=0, keepdims=True)
    row_s = jnp.sum(jnp.where(spot, col_s, 0.0), axis=0, keepdims=True)
    extra = jnp.where(row == 0, row_c, 0.0)
    extra = jnp.where(row == 1, row_s, extra)
    extra = jnp.where(row == 2, cc[TILE : TILE + 1], extra)
    extra = jnp.where(row == 3, cs[TILE : TILE + 1], extra)
    extra = jnp.where(row == 4, both[0:1], extra)
    part[0:8, :] = cc[:TILE]
    part[8:16, :] = cs[:TILE]
    part[16:24, :] = sc2
    part[24:32, :] = ss2
    part[32:40, :] = extra

    pl.semaphore_wait(rel, 1)
    second = []
    for i, step in enumerate((near, -near)):
        copy = pltpu.make_async_remote_copy(
            src_ref=part,
            dst_ref=pair.at[i],
            send_sem=s2.at[i],
            recv_sem=r2.at[i],
            device_id={"slab": at(step)},
            device_id_type=MESH,
        )
        copy.start()
        second.append(copy)

    onehot = (lax.broadcasted_iota(jnp.int32, (TILE, band), 1) == half).astype(BF16)
    lane1 = lax.broadcasted_iota(jnp.int32, (1, LANES), 1)

    def fold_one(k, carry):
        for c in range(2):
            plane = k_raw[k, c]
            p_h, p_l = split(plane)
            v_h, v_l = split(dot(fold[...], p_h) + dot(fold[...], p_l))
            u = dot(v_h, fold_t[...]) + dot(v_l, fold_t[...])
            pp, pm = u[:half, :half], u[:half, half:]
            mp, mm = u[half:, :half], u[half:, half:]
            k_fold[k, c] = pp + mm
            k_fold[k, 2 + c] = pp - mm
            k_fold[k, 4 + c] = mp + pm
            k_fold[k, 6 + c] = mp - pm
            mid = k_raw[k, c, half : half + TILE, :]
            m_h, m_l = split(mid)
            k_row[c, pl.ds(k, 1), :] = (dot(m_h, fold_t[...]) + dot(m_l, fold_t[...]))[0:1]
            n_h, n_l = split(dot_t(onehot, p_h) + dot_t(onehot, p_l))
            k_col[c, pl.ds(k, 1), :] = (dot(n_h, fold_t[...]) + dot(n_l, fold_t[...]))[0:1]
            k_zero[c, 0:1, :] = k_zero[c, 0:1, :] + jnp.where(lane1 == k, mid[0:1, half : half + 1], 0.0)
        return carry

    lax.fori_loop(0, nk // 2, fold_one, 0)

    spans = ((0, SPLIT_ROW), (SPLIT_ROW, 5 * TILE - SPLIT_ROW))
    for i, step in enumerate((near, -near)):
        second[i].wait_recv()
        copy = pltpu.make_async_remote_copy(
            src_ref=pair.at[i, pl.ds(*spans[i])],
            dst_ref=far.at[pl.ds(*spans[i])],
            send_sem=s2.at[2 + i],
            recv_sem=r2.at[2 + i],
            device_id={"slab": at(step)},
            device_id_type=MESH,
        )
        copy.start()
        second.append(copy)

    lax.fori_loop(nk // 2, nk, fold_one, 0)

    second[2].wait_recv()
    second[3].wait_recv()
    block = (((part[...] + pair[0]) + pair[1]) + far[...]) * norm
    gath[own] = block

    third, across = [], []

    def cross(slot):
        n = len(across)
        copy = pltpu.make_async_remote_copy(
            src_ref=gath.at[slot, pl.ds(0, 34)],
            dst_ref=gath.at[slot, pl.ds(0, 34)],
            send_sem=sf.at[n],
            recv_sem=rf.at[n],
            device_id={"slab": at(0, True)},
            device_id_type=MESH,
        )
        copy.start()
        across.append(copy)

    order = sorted((d for d in range(1 - reach, reach + 1) if d), key=lambda d: -abs(d))
    for i, step in enumerate(order):
        copy = pltpu.make_async_remote_copy(
            src_ref=gath.at[own, pl.ds(0, 34)],
            dst_ref=gath.at[own, pl.ds(0, 34)],
            send_sem=s3.at[i],
            recv_sem=r3.at[i],
            device_id={"slab": at(step)},
            device_id_type=MESH,
        )
        copy.start()
        third.append(copy)
    cross(own)

    r0, i0, s00 = block[34:35], -block[35:36], block[36:37]
    e_hi, e_lo = e_h[...], e_l[...]
    ur, ui = (k_col[c, :, :half] + k_col[c, :, half:] for c in range(2))
    vr, vi = (k_col[c, :, :half] - k_col[c, :, half:] for c in range(2))
    columns = (
        jnp.concatenate([ur * r0 - vi * i0, -(vi * r0 + ur * i0)], axis=1),
        jnp.concatenate([ui * r0 + vr * i0, vr * r0 - ui * i0], axis=1),
    )
    for c in range(2):
        p_h, p_l = split(columns[c])
        l0 = dot_t(e_hi, p_h) + dot_t(e_lo, p_h) + dot_t(e_hi, p_l)
        l0 = l0 + (k_zero[c, 0:1, :] * s00)[:, : l0.shape[1]]
        for k in range(nk):
            l_zero[k, c] = jnp.broadcast_to(l0[:, k : k + 1], l_zero.shape[2:])

    for i in reversed(range(len(order))):
        third[i].wait_recv()
        cross(residue(-order[i]))
    for copy in across:
        copy.wait_recv()

    planes = [gath[:, i * TILE : (i + 1) * TILE, :].reshape(half, half) for i in range(4)]
    re1 = jnp.transpose(planes[0] - planes[3])
    im1 = -jnp.transpose(planes[1] + planes[2])
    re2 = jnp.transpose(planes[0] + planes[3])
    im2 = jnp.transpose(planes[1] - planes[2])
    edges = jnp.sum(gath[:, 4 * TILE : 5 * TILE, :], axis=0)
    r0, i0 = edges[0:1], -edges[1:2]
    ur, ui = (k_row[c, :, :half] + k_row[c, :, half:] for c in range(2))
    vr, vi = (k_row[c, :, :half] - k_row[c, :, half:] for c in range(2))
    p_zero[0] = jnp.concatenate([ur * r0 - vi * i0, -(vi * r0 + ur * i0)], axis=1)
    p_zero[1] = jnp.concatenate([ui * r0 + vr * i0, vr * r0 - ui * i0], axis=1)
    acc[...] = jnp.zeros_like(acc)
    high_rows = e_h.shape[0]

    def one_kernel(k, carry):
        ur1, ui1, vr1, vi1 = k_fold[k, 0], k_fold[k, 1], k_fold[k, 2], k_fold[k, 3]
        ur2, ui2, vr2, vi2 = k_fold[k, 4], k_fold[k, 5], k_fold[k, 6], k_fold[k, 7]
        a1r, a1i = ur1 * re1 - vi1 * im1, ui1 * re1 + vr1 * im1
        a2r, a2i = ur2 * re2 - vi2 * im2, ui2 * re2 + vr2 * im2
        b1r, b1i = vr1 * re1 - ui1 * im1, vi1 * re1 + ur1 * im1
        b2r, b2i = vr2 * re2 - ui2 * im2, vi2 * re2 + ur2 * im2
        places = (
            (0, 0, a1r + a2r), (0, half, -(b1i + b2i)), (half, 0, b2i - b1i), (half, half, a2r - a1r),
            (0, band, a1i + a2i), (0, band + half, b1r + b2r), (half, band, b1r - b2r),
            (half, band + half, a2i - a1i),
        )
        for r, c, value in places:
            high, low = split(value)
            q_h[r : r + half, c : c + half] = high
            q_l[r : r + half, c : c + half] = low
        w = dot(e_h[...], q_h[...]) + dot(e_l[...], q_h[...]) + dot(e_h[...], q_l[...])
        l_re = w[:, :band] + p_zero[0, pl.ds(k, 1), :]
        l_im = w[:, band:] + p_zero[1, pl.ds(k, 1), :]
        l_h, l_l = split(jnp.concatenate([l_re, l_im], axis=0))
        f = dot(l_h, ey_h[...]) + dot(l_l, ey_h[...]) + dot(l_h, ey_l[...])
        for i in range(acc.shape[1] // LANES):
            at_lanes = slice(i * LANES, (i + 1) * LANES)
            f_re = f[:high_rows, at_lanes] + l_zero[k, 0]
            f_im = f[high_rows:, at_lanes] + l_zero[k, 1]
            acc[:, at_lanes] = acc[:, at_lanes] + (f_re * f_re + f_im * f_im)
        return carry

    lax.fori_loop(0, nk, one_kernel, 0)

    down = sum(w * acc[i : i + rows, :] for i, w in enumerate(binomial))
    image = sum(w * down[:, i : i + COLS] for i, w in enumerate(binomial))
    out_ref[...] = image * (1.0 / nk)

    for copy in first + second + third + across:
        copy.wait_send()


def tables(slabs, side, band, rows, dtype=np.float32):
    half = band // 2
    f = np.arange(1, half + 1)

    def waves(positions):
        angle = (2.0 * math.pi / side) * np.mod(np.outer(positions, f), side)
        return np.concatenate([np.cos(angle), np.sin(angle)], axis=1)

    def halves(x):
        high = x.astype(np.float32).astype(BF16)
        return high, (x - high.astype(np.float64)).astype(BF16)

    local_w = waves(np.arange(band))
    w2 = np.zeros((2 * rows, 2 * band))
    w2[:rows, :band] = local_w[:rows]
    w2[rows:, band:] = local_w[:rows]
    edge_rows = -(-(rows + 4) // 8) * 8
    columns = np.zeros((band, -(-(COLS + 4) // LANES) * LANES))
    columns[:, : COLS + 4] = waves(np.arange(COLS + 4) - 2).T
    fold = np.zeros((band, band), np.float32)
    for i in range(half):
        if i + 1 < half:
            fold[i, half + 1 + i] = 1.0
        fold[half + i, half - 1 - i] = 1.0
    return (
        *halves(local_w),
        waves(band * np.arange(side // band)).astype(np.float32),
        *halves(w2),
        waves(rows * np.arange(slabs)).astype(np.float32),
        waves(np.arange(edge_rows) - 2).astype(np.float32),
        *halves(columns),
        fold.astype(BF16),
        fold.T.astype(BF16),
    )


def local(transmission, kernel_spectra):
    rows, side = transmission.shape
    nk, _, band, _ = kernel_spectra.shape
    slabs = lax.axis_size("slab")
    half = band // 2
    blocks = half // TILE
    constants = tables(slabs, side, band, rows)
    edge_rows = constants[6].shape[0]
    wide = constants[7].shape[1]
    nk_pad = -(-nk // 8) * 8
    vmem = pl.BlockSpec(memory_space=pltpu.VMEM)
    sends1, sends3 = blocks - 1, blocks // 2 - 1
    dma = pltpu.SemaphoreType.DMA
    return pl.pallas_call(
        functools.partial(image_kernel, (slabs, side, band, nk, rows)),
        out_shape=jax.ShapeDtypeStruct((rows, COLS), F32),
        in_specs=[vmem, pl.BlockSpec(memory_space=pl.ANY)] + [vmem] * len(constants),
        out_specs=vmem,
        scratch_shapes=[
            pltpu.VMEM(kernel_spectra.shape, F32),
            pltpu.VMEM((nk, 8, half, half), F32),
            pltpu.VMEM((2, nk_pad, band), F32),
            pltpu.VMEM((2, nk_pad, band), F32),
            pltpu.VMEM((2, TILE, LANES), F32),
            pltpu.VMEM((rows * side // band, band), BF16),
            pltpu.VMEM((rows * side // band, band), BF16),
            pltpu.VMEM((blocks, 2 * TILE, LANES), F32),
            pltpu.VMEM((blocks, 2 * TILE, LANES), F32),
            pltpu.VMEM((5 * TILE, LANES), F32),
            pltpu.VMEM((2, 5 * TILE, LANES), F32),
            pltpu.VMEM((5 * TILE, LANES), F32),
            pltpu.VMEM((blocks, 5 * TILE, LANES), F32),
            pltpu.VMEM((edge_rows, band), BF16),
            pltpu.VMEM((edge_rows, band), BF16),
            pltpu.VMEM((nk, 2, edge_rows, LANES), F32),
            pltpu.VMEM((2, nk_pad, band), F32),
            pltpu.VMEM((band, 2 * band), BF16),
            pltpu.VMEM((band, 2 * band), BF16),
            pltpu.VMEM((edge_rows, wide), F32),
            dma(()),
            dma((sends1,)),
            dma((sends1,)),
            dma((4,)),
            dma((4,)),
            dma((sends3,)),
            dma((sends3,)),
            dma((sends3 + 1,)),
            dma((sends3 + 1,)),
            pltpu.SemaphoreType.REGULAR,
        ],
        compiler_params=pltpu.CompilerParams(
            collective_id=0, has_side_effects=True, vmem_limit_bytes=60 * 1024 * 1024
        ),
        name="aerial_image",
    )(transmission, kernel_spectra, *constants)


def solution(mesh):
    return jax.shard_map(
        local,
        mesh=mesh,
        in_specs=(P(("tiles", "slab"), None), P()),
        out_specs=P(("tiles", "slab"), None),
        check_vma=False,
    )
```

profile of v0, /device:TPU:37, one launch (start us, length us, event | category | flops | bytes accessed | tf_op | source)
XLA Modules:
  0.0 65.3 jit_solution(13355861166112973953)
XLA Ops:
  0.0 63.8 %aerial_image.1 = f32[64,256]{1,0:T(8,128)} custom-call(f32[64,4096]{1,0:T(8,128)} %t_ref.1, f32[12,2,256,256]{3,2,1,0:T(8,128)} %k_hbm.1, bf16[256,256]{1,0:T(8,128)(2,1)} %constant.22.clone.wy_h, bf16[256,256]{1,0:T(8,128)(2,1)} %constant.23.clone.wy_l, f32[16,256]{1,0:T(8,128)} %constant.24.clone.tw_chunk, bf16[128,512]{1,0:T(8,128)(2,1)} %constant.25.clone.w2_h, ...), custom_call_target="tpu_custom_call" | custom-call | tf_op jit(solution)/shard_map/aerial_image/pallas_call | solution.py:394
  63.9 1.5 %copy.15 = f32[64,256]{1,0:T(8,128)} copy(f32[64,256]{1,0:T(8,128)} %aerial_image.1) | data formatting | bytes 131072
where the time goes:
time: 65.5 us; the launch traced here: 65.3 us
  Pallas kernels  63.8 us (97%)
  local copies, waits for them, and re-layouts  1.47 us (2%)
    pallas_call x1, Pallas kernels, local(): pl.pallas_call(functools.partial(image_kernel, (slabs, side, band, nk, ro...  63.8 us
    unnamed x1, local copies, waits for them, and re-layouts  1.47 us

commit v1 on v0

--- a/solution.py
+++ b/solution.py
@@ -13,7 +13,7 @@
 MESH = pl.DeviceIdType.MESH
 F32, BF16 = jnp.float32, jnp.bfloat16
 LANES, TILE = 128, 8
-SPLIT_ROW = 24
+SPLIT_ROW, PART_ROWS = 24, 37
 
 binomial = (0.0625, 0.25, 0.375, 0.25, 0.0625)
 
@@ -33,11 +33,12 @@
 
 def image_kernel(
     sizes,
-    t_ref, k_hbm, wy_h, wy_l, tw_chunk, w2_h, w2_l, tw_slab, e_local, ey_h, ey_l, fold, fold_t,
+    t_hbm, k_hbm, plain_hbm, near_hbm, half_hbm, wide_hbm,
     out_ref,
+    t_ref, plain, near_w, halves_w, wide_w,
     k_raw, k_fold, k_row, k_col, k_zero, t_h, t_l, z_ref, slots, part, pair, far, gath,
-    e_h, e_l, l_zero, p_zero, q_h, q_l, acc,
-    k_sem, s1, r1, s2, r2, s3, r3, sf, rf, rel,
+    e_h, e_l, l_zero, p_zero, q_h, q_l, l_h, l_l, acc,
+    in_sem, t_sem, s1, r1, s2, r2, s3, r3, sf, rf, rel,
 ):
     slabs, side, band, nk, rows = sizes
     half = band // 2
@@ -56,9 +57,6 @@
     def residue(step, other=False):
         c = 1 - core if other else core
         return 2 * lax.rem(chip + step + slabs, near) + c
-
-    load = pltpu.make_async_copy(k_hbm, k_raw, k_sem)
-    load.start()
 
     barrier = pltpu.get_barrier_semaphore()
     reach = near // 2
@@ -73,10 +71,36 @@
 
     chunks = side // band
     group = 4
+    span = group * band
+    loads = [
+        pltpu.make_async_copy(a, b, in_sem.at[i])
+        for i, (a, b) in enumerate(
+            ((near_hbm, near_w), (plain_hbm, plain), (half_hbm, halves_w), (wide_hbm, wide_w), (k_hbm, k_raw))
+        )
+    ]
+    pieces = [
+        pltpu.make_async_copy(
+            t_hbm.at[:, pl.ds(g * span, span)], t_ref.at[:, pl.ds(g * span, span)], t_sem.at[g]
+        )
+        for g in range(chunks // group)
+    ]
+    for copy in pieces[:1] + loads[:2] + pieces[1:] + loads[2:]:
+        copy.start()
+    tw_chunk = plain.at[0:chunks]
+    tw_slab = plain.at[chunks : chunks + slabs]
+    e_local = plain.at[chunks + slabs :]
+    wy_h, wy_l = near_w.at[0:band], near_w.at[band:]
+    w2_h, w2_l = halves_w.at[0 : 2 * rows], halves_w.at[2 * rows : 4 * rows]
+    fold, fold_t = halves_w.at[4 * rows : 4 * rows + band, 0:band], halves_w.at[4 * rows : 4 * rows + band, band:]
+    ey_h, ey_l = wide_w.at[0:band], wide_w.at[band:]
+
+    loads[0].wait()
+    loads[1].wait()
     sum_c = jnp.zeros((rows, half), F32)
     sum_s = jnp.zeros((rows, half), F32)
     row_sum = jnp.zeros((rows, LANES), F32)
     for g in range(chunks // group):
+        pieces[g].wait()
         for j in range(group):
             h = g * group + j
             piece = t_ref[:, h * band : (h + 1) * band]
@@ -137,11 +161,38 @@
     sc, ss = tw_slab[0:blocks, :half], tw_slab[0:blocks, half:]
     wc, ws = bc * sc - bs * ss, bc * ss + bs * sc
 
-    load.wait()
+    onehot = (lax.broadcasted_iota(jnp.int32, (TILE, band), 1) == half).astype(BF16)
+    lane1 = lax.broadcasted_iota(jnp.int32, (1, LANES), 1)
+    k_zero[...] = jnp.zeros_like(k_zero)
+
+    def fold_one(k, carry):
+        for c in range(2):
+            plane = k_raw[k, c]
+            p_h, p_l = split(plane)
+            v_h, v_l = split(dot(fold[...], p_h) + dot(fold[...], p_l))
+            u = dot(v_h, fold_t[...]) + dot(v_l, fold_t[...])
+            pp, pm = u[:half, :half], u[:half, half:]
+            mp, mm = u[half:, :half], u[half:, half:]
+            k_fold[k, c] = pp + mm
+            k_fold[k, 2 + c] = pp - mm
+            k_fold[k, 4 + c] = mp + pm
+            k_fold[k, 6 + c] = mp - pm
+            mid = k_raw[k, c, half : half + TILE, :]
+            m_h, m_l = split(mid)
+            k_row[c, pl.ds(k, 1), :] = (dot(m_h, fold_t[...]) + dot(m_l, fold_t[...]))[0:1]
+            n_h, n_l = split(dot_t(onehot, p_h) + dot_t(onehot, p_l))
+            k_col[c, pl.ds(k, 1), :] = (dot(n_h, fold_t[...]) + dot(n_l, fold_t[...]))[0:1]
+            k_zero[c, 0:1, :] = k_zero[c, 0:1, :] + jnp.where(lane1 == k, mid[0:1, half : half + 1], 0.0)
+        return carry
+
+    for copy in loads[2:]:
+        copy.wait()
+    cuts = (0, nk // 4, nk // 4 + (5 * nk) // 12, nk)
+    lax.fori_loop(cuts[0], cuts[1], fold_one, 0)
+
     for copy in first:
         copy.wait_recv()
 
-    k_zero[...] = jnp.zeros_like(k_zero)
     everything = slots[...]
     a_h, a_l = split(everything.reshape(blocks * 2 * TILE, LANES))
     y = dot(a_h, w2_h[...]) + dot(a_l, w2_h[...]) + dot(a_h, w2_l[...])
@@ -181,62 +232,41 @@
     part[32:40, :] = extra
 
     pl.semaphore_wait(rel, 1)
+    spans = ((0, SPLIT_ROW), (SPLIT_ROW, PART_ROWS - SPLIT_ROW))
     second = []
-    for i, step in enumerate((near, -near)):
-        copy = pltpu.make_async_remote_copy(
-            src_ref=part,
-            dst_ref=pair.at[i],
-            send_sem=s2.at[i],
-            recv_sem=r2.at[i],
-            device_id={"slab": at(step)},
-            device_id_type=MESH,
-        )
-        copy.start()
-        second.append(copy)
-
-    onehot = (lax.broadcasted_iota(jnp.int32, (TILE, band), 1) == half).astype(BF16)
-    lane1 = lax.broadcasted_iota(jnp.int32, (1, LANES), 1)
-
-    def fold_one(k, carry):
-        for c in range(2):
-            plane = k_raw[k, c]
-            p_h, p_l = split(plane)
-            v_h, v_l = split(dot(fold[...], p_h) + dot(fold[...], p_l))
-            u = dot(v_h, fold_t[...]) + dot(v_l, fold_t[...])
-            pp, pm = u[:half, :half], u[:half, half:]
-            mp, mm = u[half:, :half], u[half:, half:]
-            k_fold[k, c] = pp + mm
-            k_fold[k, 2 + c] = pp - mm
-            k_fold[k, 4 + c] = mp + pm
-            k_fold[k, 6 + c] = mp - pm
-            mid = k_raw[k, c, half : half + TILE, :]
-            m_h, m_l = split(mid)
-            k_row[c, pl.ds(k, 1), :] = (dot(m_h, fold_t[...]) + dot(m_l, fold_t[...]))[0:1]
-            n_h, n_l = split(dot_t(onehot, p_h) + dot_t(onehot, p_l))
-            k_col[c, pl.ds(k, 1), :] = (dot(n_h, fold_t[...]) + dot(n_l, fold_t[...]))[0:1]
-            k_zero[c, 0:1, :] = k_zero[c, 0:1, :] + jnp.where(lane1 == k, mid[0:1, half : half + 1], 0.0)
-        return carry
-
-    lax.fori_loop(0, nk // 2, fold_one, 0)
-
-    spans = ((0, SPLIT_ROW), (SPLIT_ROW, 5 * TILE - SPLIT_ROW))
+    for turn in range(2):
+        for i, step in enumerate((near, -near)):
+            span = spans[i] if turn == 0 else spans[1 - i]
+            copy = pltpu.make_async_remote_copy(
+                src_ref=part.at[pl.ds(*span)],
+                dst_ref=pair.at[i, pl.ds(*span)],
+                send_sem=s2.at[2 * turn + i],
+                recv_sem=r2.at[2 * turn + i],
+                device_id={"slab": at(step)},
+                device_id_type=MESH,
+            )
+            copy.start()
+            second.append(copy)
+
+    lax.fori_loop(cuts[1], cuts[2], fold_one, 0)
+
     for i, step in enumerate((near, -near)):
         second[i].wait_recv()
         copy = pltpu.make_async_remote_copy(
             src_ref=pair.at[i, pl.ds(*spans[i])],
             dst_ref=far.at[pl.ds(*spans[i])],
-            send_sem=s2.at[2 + i],
-            recv_sem=r2.at[2 + i],
+            send_sem=s2.at[4 + i],
+            recv_sem=r2.at[4 + i],
             device_id={"slab": at(step)},
             device_id_type=MESH,
         )
         copy.start()
         second.append(copy)
 
-    lax.fori_loop(nk // 2, nk, fold_one, 0)
-
-    second[2].wait_recv()
-    second[3].wait_recv()
+    lax.fori_loop(cuts[2], cuts[3], fold_one, 0)
+
+    for copy in second[2:]:
+        copy.wait_recv()
     block = (((part[...] + pair[0]) + pair[1]) + far[...]) * norm
     gath[own] = block
 
@@ -301,10 +331,9 @@
     vr, vi = (k_row[c, :, :half] - k_row[c, :, half:] for c in range(2))
     p_zero[0] = jnp.concatenate([ur * r0 - vi * i0, -(vi * r0 + ur * i0)], axis=1)
     p_zero[1] = jnp.concatenate([ui * r0 + vr * i0, vr * r0 - ui * i0], axis=1)
-    acc[...] = jnp.zeros_like(acc)
     high_rows = e_h.shape[0]
 
-    def one_kernel(k, carry):
+    def products(k):
         ur1, ui1, vr1, vi1 = k_fold[k, 0], k_fold[k, 1], k_fold[k, 2], k_fold[k, 3]
         ur2, ui2, vr2, vi2 = k_fold[k, 4], k_fold[k, 5], k_fold[k, 6], k_fold[k, 7]
         a1r, a1i = ur1 * re1 - vi1 * im1, ui1 * re1 + vr1 * im1
@@ -318,21 +347,33 @@
         )
         for r, c, value in places:
             high, low = split(value)
-            q_h[r : r + half, c : c + half] = high
-            q_l[r : r + half, c : c + half] = low
-        w = dot(e_h[...], q_h[...]) + dot(e_l[...], q_h[...]) + dot(e_h[...], q_l[...])
-        l_re = w[:, :band] + p_zero[0, pl.ds(k, 1), :]
-        l_im = w[:, band:] + p_zero[1, pl.ds(k, 1), :]
-        l_h, l_l = split(jnp.concatenate([l_re, l_im], axis=0))
-        f = dot(l_h, ey_h[...]) + dot(l_l, ey_h[...]) + dot(l_h, ey_l[...])
+            q_h[k, r : r + half, c : c + half] = high
+            q_l[k, r : r + half, c : c + half] = low
+
+    def over_x(k):
+        w = dot(e_h[...], q_h[k]) + dot(e_l[...], q_h[k]) + dot(e_h[...], q_l[k])
+        l_re = w[:, :band] + p_zero[0, k : k + 1, :]
+        l_im = w[:, band:] + p_zero[1, k : k + 1, :]
+        high, low = split(jnp.concatenate([l_re, l_im], axis=0))
+        l_h[k] = high
+        l_l[k] = low
+
+    def over_y(k):
+        f = dot(l_h[k], ey_h[...]) + dot(l_l[k], ey_h[...]) + dot(l_h[k], ey_l[...])
         for i in range(acc.shape[1] // LANES):
             at_lanes = slice(i * LANES, (i + 1) * LANES)
             f_re = f[:high_rows, at_lanes] + l_zero[k, 0]
             f_im = f[high_rows:, at_lanes] + l_zero[k, 1]
-            acc[:, at_lanes] = acc[:, at_lanes] + (f_re * f_re + f_im * f_im)
-        return carry
-
-    lax.fori_loop(0, nk, one_kernel, 0)
+            power = f_re * f_re + f_im * f_im
+            acc[:, at_lanes] = acc[:, at_lanes] + power if k else power
+
+    for k in range(nk + 2):
+        if k < nk:
+            products(k)
+        if 0 <= k - 1 < nk:
+            over_x(k - 1)
+        if k >= 2:
+            over_y(k - 2)
 
     down = sum(w * acc[i : i + rows, :] for i, w in enumerate(binomial))
     image = sum(w * down[:, i : i + COLS] for i, w in enumerate(binomial))
@@ -366,15 +407,15 @@
         if i + 1 < half:
             fold[i, half + 1 + i] = 1.0
         fold[half + i, half - 1 - i] = 1.0
+    plain = np.concatenate(
+        [waves(band * np.arange(side // band)), waves(rows * np.arange(slabs)), waves(np.arange(edge_rows) - 2)]
+    ).astype(np.float32)
+    folds = np.concatenate([fold, fold.T], axis=1).astype(BF16)
     return (
-        *halves(local_w),
-        waves(band * np.arange(side // band)).astype(np.float32),
-        *halves(w2),
-        waves(rows * np.arange(slabs)).astype(np.float32),
-        waves(np.arange(edge_rows) - 2).astype(np.float32),
-        *halves(columns),
-        fold.astype(BF16),
-        fold.T.astype(BF16),
+        plain,
+        np.concatenate(halves(local_w)),
+        np.concatenate([*halves(w2), folds]),
+        np.concatenate(halves(columns)),
     )
 
 
@@ -385,18 +426,20 @@
     half = band // 2
     blocks = half // TILE
     constants = tables(slabs, side, band, rows)
-    edge_rows = constants[6].shape[0]
-    wide = constants[7].shape[1]
+    edge_rows = constants[0].shape[0] - slabs - side // band
+    wide = constants[3].shape[1]
     nk_pad = -(-nk // 8) * 8
     vmem = pl.BlockSpec(memory_space=pltpu.VMEM)
     sends1, sends3 = blocks - 1, blocks // 2 - 1
     dma = pltpu.SemaphoreType.DMA
     return pl.pallas_call(
         functools.partial(image_kernel, (slabs, side, band, nk, rows)),
-        out_shape=jax.ShapeDtypeStruct((rows, COLS), F32),
-        in_specs=[vmem, pl.BlockSpec(memory_space=pl.ANY)] + [vmem] * len(constants),
+        out_shape=pltpu.VMEM((rows, COLS), F32),
+        in_specs=[pl.BlockSpec(memory_space=pl.ANY)] * (2 + len(constants)),
         out_specs=vmem,
         scratch_shapes=[
+            pltpu.VMEM((rows, side), F32),
+            *(pltpu.VMEM(c.shape, c.dtype) for c in constants),
             pltpu.VMEM(kernel_spectra.shape, F32),
             pltpu.VMEM((nk, 8, half, half), F32),
             pltpu.VMEM((2, nk_pad, band), F32),
@@ -414,14 +457,17 @@
             pltpu.VMEM((edge_rows, band), BF16),
             pltpu.VMEM((nk, 2, edge_rows, LANES), F32),
             pltpu.VMEM((2, nk_pad, band), F32),
-            pltpu.VMEM((band, 2 * band), BF16),
-            pltpu.VMEM((band, 2 * band), BF16),
+            pltpu.VMEM((nk, band, 2 * band), BF16),
+            pltpu.VMEM((nk, band, 2 * band), BF16),
+            pltpu.VMEM((nk, 2 * edge_rows, band), BF16),
+            pltpu.VMEM((nk, 2 * edge_rows, band), BF16),
             pltpu.VMEM((edge_rows, wide), F32),
-            dma(()),
+            dma((5,)),
+            dma((side // band // 4,)),
             dma((sends1,)),
             dma((sends1,)),
-            dma((4,)),
-            dma((4,)),
+            dma((6,)),
+            dma((6,)),
             dma((sends3,)),
             dma((sends3,)),
             dma((sends3 + 1,)),

time: 65.5 us -> 56.7 us (0.87)
  Pallas kernels: 63.8 us -> 55.9 us
  local copies, waits for them, and re-layouts: 1.47 us -> 0.63 us
    pallas_call x1, Pallas kernels: 63.8 us -> 55.9 us  [local(): pl.pallas_call(functools.partial(image_kernel, (slabs, side, band, nk, ro...]
    unnamed x1, local copies, waits for them, and re-layouts: 1.47 us -> 0.63 us
where the time goes in v1:
time: 56.7 us; the launch traced here: 56.6 us
  Pallas kernels  55.9 us (99%)
  local copies, waits for them, and re-layouts  0.63 us (1%)
    pallas_call x1, Pallas kernels, local(): pl.pallas_call(functools.partial(image_kernel, (slabs, side, band, nk, ro...  55.9 us

profile of v1, /device:TPU:37, one launch (start us, length us, event | category | flops | bytes accessed | tf_op | source)
XLA Modules:
  0.0 56.6 jit_solution(13974127354522688192)
XLA Ops:
  0.0 55.9 %aerial_image.1 = f32[64,256]{1,0:T(8,128)S(1)} custom-call(f32[64,4096]{1,0:T(8,128)} %t_hbm.1, f32[12,2,256,256]{3,2,1,0:T(8,128)} %k_hbm.1, f32[152,256]{1,0:T(8,128)} %constant.8.clone.plain_hbm, bf16[512,256]{1,0:T(8,128)(2,1)} %constant.9.clone.near_hbm, bf16[512,512]{1,0:T(8,128)(2,1)} %constant.10.clone.half_hbm, ...), custom_call_target="tpu_custom_call" | custom-call | tf_op jit(solution)/shard_map/aerial_image/pallas_call | solution.py:435
  55.9 0.6 %copy.8 = f32[64,256]{1,0:T(8,128)} copy(f32[64,256]{1,0:T(8,128)S(1)} %aerial_image.1) | data formatting | bytes 131072
